TPU v7x, 16 devices: a whole 2x2x2 slice. The times are simulated.
16 devices in a mesh: fsdp: 16 (over z, y, x, core).
Axes of the slice: x: 2, y: 2, z: 2, core: 2. Of those that a mesh axis runs over, the one named last changes fastest.
Arguments:
- x: bfloat16 [4, 65536, 768], P(None, 'fsdp')
- g: bfloat16 [4, 65536, 768], P(None, 'fsdp')
- w1: bfloat16 [1, 768, 3072], P(None, 'fsdp')
- w2: bfloat16 [1, 3072, 768], P(None, 'fsdp')
Outputs:
- output 1: bfloat16 [4, 65536, 768], P(None, 'fsdp')
- output 2: float32 [1, 768, 3072], P(None, 'fsdp')
- output 3: float32 [1, 3072, 768], P(None, 'fsdp')
All inputs are finite; a program needn't handle non-finite values.
Results may differ from a plain program's by a relative error of at most 0.00940272.
Values are sent between devices in bfloat16 or wider.
A program may use at most 1 GiB of HBM per device.

v0:
```python
import jax
import jax.numpy as jnp
from jax import lax
from jax.sharding import PartitionSpec as P

AX = "fsdp"


def _gelu_bwd(a, e):
    return jax.vjp(jax.nn.gelu, a)[1](e)[0]


def solution(mesh):
    spec = P(None, AX, None)

    def body(x, g, w1, w2):
        layers = w1.shape[0]

        def micro(acc, xg):
            cur, gy = xg
            saved = []
            for l in range(layers):
                v1 = lax.all_gather(w1[l], AX, axis=0, tiled=True)
                v2 = lax.all_gather(w2[l], AX, axis=0, tiled=True)
                a = jnp.dot(cur, v1, preferred_element_type=jnp.float32).astype(jnp.bfloat16)
                h = jax.nn.gelu(a.astype(jnp.float32)).astype(jnp.bfloat16)
                saved.append((cur, a))
                cur = (cur.astype(jnp.float32) + jnp.dot(h, v2, preferred_element_type=jnp.float32)).astype(jnp.bfloat16)
            d1, d2 = [None] * layers, [None] * layers
            for l in reversed(range(layers)):
                xl, a = saved[l]
                v2 = lax.all_gather(w2[l], AX, axis=0, tiled=True)
                h = jax.nn.gelu(a.astype(jnp.float32)).astype(jnp.bfloat16)
                e = jnp.dot(gy, v2.T, preferred_element_type=jnp.float32)
                da = _gelu_bwd(a.astype(jnp.float32), e).astype(jnp.bfloat16)
                p2 = jnp.dot(h.T, gy, preferred_element_type=jnp.float32)
                p1 = jnp.dot(xl.T, da, preferred_element_type=jnp.float32)
                d2[l] = acc[1][l] + lax.psum_scatter(p2, AX, scatter_dimension=0, tiled=True)
                d1[l] = acc[0][l] + lax.psum_scatter(p1, AX, scatter_dimension=0, tiled=True)
                if l > 0:
                    v1 = lax.all_gather(w1[l], AX, axis=0, tiled=True)
                    gy = (gy.astype(jnp.float32) + jnp.dot(da, v1.T, preferred_element_type=jnp.float32)).astype(jnp.bfloat16)
            return (jnp.stack(d1), jnp.stack(d2)), cur

        zeros = (jnp.zeros(w1.shape, jnp.float32), jnp.zeros(w2.shape, jnp.float32))
        (d1, d2), y = lax.scan(micro, zeros, (x, g))
        return y, d1, d2

    return jax.shard_map(body, mesh=mesh, in_specs=(spec, spec, spec, spec),
                         out_specs=(spec, spec, spec), check_vma=False)
```

profile of v0, /device:TPU:0, one launch (start us, length us, event | category | flops | bytes accessed | tf_op | source)
XLA Modules:
  0.0 1078.9 jit_solution(11474066354046439841)
XLA Ops:
  7.2 0.9 broadcast_in_dim.17
  8.0 0.9 broadcast_in_dim.16
  8.9 1063.4 %while.16 = (s32[]{:T(128)}, f32[1,48,3072]{2,1,0:T(8,128)}, f32[1,192,768]{2,1,0:T(8,128)}, bf16[4,4096,768]{2,1,0:T(8,128)(2,1)}, bf16[4,4096,768]{2,1,0:T(8,1...) while((s32[]{:T(128)}, f32[1,48,3072]{2,1,0:T(8,128)}, ...), condition=%wide.region_3.4_spmd, body=%wide.region_0.3_spmd.sunk | while | flops 97174978560 | bytes 324993408 | solution.py:46
  8.9 0.7 all-gather.9.cloned.1.call-update
  9.6 0.0 all-gather.11.cloned.1.call-start
  9.6 0.7 all-gather.11.cloned.1.call-update
  10.4 0.0 reduce-scatter.5.cloned.1.call-start
  10.4 41.0 %all-gather.9.cloned.1.call-done = bf16[1,768,3072]{2,1,0:T(8,128)(2,1)} async-done(((bf16[1,48,3072]{2,1,0:T(8,128)(2,1)}), bf16[1,768,3072]{2,1,0:T(8,128)(2,1)}) %all-gather.9.cloned.1.call-update) | async-done | bytes 4718608 | tf_op jit(solution)/shard_map/while/body/eval_jaxpr/all_gather | solution.py:23
  51.4 26.9 %convolution_convert_fusion.2 = bf16[4096,3072]{1,0:T(8,128)(2,1)} fusion(bf16[4,4096,768]{2,1,0:T(8,128)(2,1)} %get-tuple-element.196, s32[]{:T(128)S(6)} %copy.12, bf16[1,768,3072]{2,1,0:T(8,128)(2,1)} %all-gather.9.cloned.1.call-done), kind=kOutput, calls=%fused_computation.17.clone.1 | convolution fusion | flops 19339935744 | bytes 36175876 | tf_op jit(solution)/shard_map/while/body/eval_jaxpr/dot_general | solution.py:25
  78.3 32.9 %fusion.87 = f32[3072,768]{1,0:T(8,128)} fusion(bf16[4,4096,768]{2,1,0:T(8,128)(2,1)} %get-tuple-element.197, s32[]{:T(128)S(6)} %copy.12, bf16[4096,3072]{1,0:T(8,128)(2,1)} %convolution_convert_fusion.2), kind=kOutput, calls=%fused_computation.20.clone.1 | convolution fusion | flops 19453181952 | bytes 40894468 | tf_op jit(solution)/shard_map/while/body/eval_jaxpr/dot_general | solution.py:36
  111.2 0.0 reduce-scatter.3.cloned.1.call-start
  111.3 0.0 all-gather.11.cloned.1.call-done
  111.3 57.4 %fusion.84 = bf16[4096,3072]{1,0:T(8,128)(2,1)} fusion(bf16[4096,3072]{1,0:T(8,128)(2,1)} %convolution_convert_fusion.2, bf16[4,4096,768]{2,1,0:T(8,128)(2,1)} %get-tuple-element.197, s32[]{:T(128)S(6)} %copy.12, bf16[1,3072,768]{2,1,0:T(8,128)(2,1)} %all-gather.11.cloned.1.call-done), kind=kOutput, calls=%fused_computation.8.clone.clone.2.clone.1 | convolution fusion | flops 19591593984 | bytes 61341700 | tf_op jit(solution)/shard_map/while/body/eval_jaxpr/dot_general | solution.py:34
  168.7 26.6 %fusion.85 = f32[768,3072]{1,0:T(8,128)} fusion(s32[]{:T(128)S(6)} %copy.12, bf16[4,4096,768]{2,1,0:T(8,128)(2,1)} %get-tuple-element.196, bf16[4096,3072]{1,0:T(8,128)(2,1)} %fusion.84), kind=kOutput, calls=%fused_computation.15.clone.3 | convolution fusion | flops 19327352832 | bytes 40894468 | tf_op jit(solution)/shard_map/while/body/eval_jaxpr/dot_general | solution.py:37
  195.3 36.8 %bitcast_dynamic-update-slice_fusion.2 = bf16[4,4096,768]{2,1,0:T(8,128)(2,1)} fusion(bf16[4,4096,768]{2,1,0:T(8,128)(2,1)} %get-tuple-element.186, s32[]{:T(128)S(6)} %copy.12, bf16[4,4096,768]{2,1,0:T(8,128)(2,1)} %get-tuple-element.196, bf16[1,3072,768]{2,1,0:T(8,128)(2,1)} %all-gather.11.cloned.1.call-done, ...), kind=kOutput, calls=%fused_computation.19.clone.1 | convolution fusion | flops 19462619136 | bytes 42467332 | tf_op jit(solution)/shard_map/while/body/eval_jaxpr/dot_general | solution.py:28
  232.2 1.2 fusion.88
  233.4 41.5 %reduce-scatter.3.cloned.1.call-done = f32[48,3072]{1,0:T(8,128)} async-done(((f32[768,3072]{1,0:T(8,128)}), f32[48,3072]{1,0:T(8,128)}) %reduce-scatter.3.cloned.1.call-update) | async-done | bytes 589840 | tf_op jit(solution)/shard_map/while/body/eval_jaxpr/reduce_scatter | solution.py:39
  274.9 1.2 fusion.86
  276.1 0.8 copy-done.3
  276.9 0.6 all-gather.9.cloned.1.call-update
  277.5 0.0 all-gather.11.cloned.1.call-start
  277.5 0.5 all-gather.11.cloned.1.call-update
  278.1 0.0 reduce-scatter.5.cloned.1.call-start
  278.1 38.2 %all-gather.9.cloned.1.call-done = bf16[1,768,3072]{2,1,0:T(8,128)(2,1)} async-done(((bf16[1,48,3072]{2,1,0:T(8,128)(2,1)}), bf16[1,768,3072]{2,1,0:T(8,128)(2,1)}) %all-gather.9.cloned.1.call-update) | async-done | bytes 4718608 | tf_op jit(solution)/shard_map/while/body/eval_jaxpr/all_gather | solution.py:23
  316.3 26.9 %convolution_convert_fusion.2 = bf16[4096,3072]{1,0:T(8,128)(2,1)} fusion(bf16[4,4096,768]{2,1,0:T(8,128)(2,1)} %get-tuple-element.196, s32[]{:T(128)S(6)} %copy.12, bf16[1,768,3072]{2,1,0:T(8,128)(2,1)} %all-gather.9.cloned.1.call-done), kind=kOutput, calls=%fused_computation.17.clone.1 | convolution fusion | flops 19339935744 | bytes 36175876 | tf_op jit(solution)/shard_map/while/body/eval_jaxpr/dot_general | solution.py:25
  343.2 32.9 %fusion.87 = f32[3072,768]{1,0:T(8,128)} fusion(bf16[4,4096,768]{2,1,0:T(8,128)(2,1)} %get-tuple-element.197, s32[]{:T(128)S(6)} %copy.12, bf16[4096,3072]{1,0:T(8,128)(2,1)} %convolution_convert_fusion.2), kind=kOutput, calls=%fused_computation.20.clone.1 | convolution fusion | flops 19453181952 | bytes 40894468 | tf_op jit(solution)/shard_map/while/body/eval_jaxpr/dot_general | solution.py:36
  376.2 0.0 reduce-scatter.3.cloned.1.call-start
  376.2 57.4 %fusion.84 = bf16[4096,3072]{1,0:T(8,128)(2,1)} fusion(bf16[4096,3072]{1,0:T(8,128)(2,1)} %convolution_convert_fusion.2, bf16[4,4096,768]{2,1,0:T(8,128)(2,1)} %get-tuple-element.197, s32[]{:T(128)S(6)} %copy.12, bf16[1,3072,768]{2,1,0:T(8,128)(2,1)} %all-gather.11.cloned.1.call-done), kind=kOutput, calls=%fused_computation.8.clone.clone.2.clone.1 | convolution fusion | flops 19591593984 | bytes 61341700 | tf_op jit(solution)/shard_map/while/body/eval_jaxpr/dot_general | solution.py:34
  433.6 26.6 %fusion.85 = f32[768,3072]{1,0:T(8,128)} fusion(s32[]{:T(128)S(6)} %copy.12, bf16[4,4096,768]{2,1,0:T(8,128)(2,1)} %get-tuple-element.196, bf16[4096,3072]{1,0:T(8,128)(2,1)} %fusion.84), kind=kOutput, calls=%fused_computation.15.clone.3 | convolution fusion | flops 19327352832 | bytes 40894468 | tf_op jit(solution)/shard_map/while/body/eval_jaxpr/dot_general | solution.py:37
  460.3 36.8 %bitcast_dynamic-update-slice_fusion.2 = bf16[4,4096,768]{2,1,0:T(8,128)(2,1)} fusion(bf16[4,4096,768]{2,1,0:T(8,128)(2,1)} %get-tuple-element.186, s32[]{:T(128)S(6)} %copy.12, bf16[4,4096,768]{2,1,0:T(8,128)(2,1)} %get-tuple-element.196, bf16[1,3072,768]{2,1,0:T(8,128)(2,1)} %all-gather.11.cloned.1.call-done, ...), kind=kOutput, calls=%fused_computation.19.clone.1 | convolution fusion | flops 19462619136 | bytes 42467332 | tf_op jit(solution)/shard_map/while/body/eval_jaxpr/dot_general | solution.py:28
  497.1 1.2 fusion.88
  498.3 41.6 %reduce-scatter.3.cloned.1.call-done = f32[48,3072]{1,0:T(8,128)} async-done(((f32[768,3072]{1,0:T(8,128)}), f32[48,3072]{1,0:T(8,128)}) %reduce-scatter.3.cloned.1.call-update) | async-done | bytes 589840 | tf_op jit(solution)/shard_map/while/body/eval_jaxpr/reduce_scatter | solution.py:39
  539.9 1.2 fusion.86
  541.1 0.8 copy-done.3
  541.9 0.7 all-gather.9.cloned.1.call-update
  542.6 0.0 all-gather.11.cloned.1.call-start
  542.7 0.5 all-gather.11.cloned.1.call-update
  543.2 0.0 reduce-scatter.5.cloned.1.call-start
  543.3 38.3 %all-gather.9.cloned.1.call-done = bf16[1,768,3072]{2,1,0:T(8,128)(2,1)} async-done(((bf16[1,48,3072]{2,1,0:T(8,128)(2,1)}), bf16[1,768,3072]{2,1,0:T(8,128)(2,1)}) %all-gather.9.cloned.1.call-update) | async-done | bytes 4718608 | tf_op jit(solution)/shard_map/while/body/eval_jaxpr/all_gather | solution.py:23
  581.6 26.9 %convolution_convert_fusion.2 = bf16[4096,3072]{1,0:T(8,128)(2,1)} fusion(bf16[4,4096,768]{2,1,0:T(8,128)(2,1)} %get-tuple-element.196, s32[]{:T(128)S(6)} %copy.12, bf16[1,768,3072]{2,1,0:T(8,128)(2,1)} %all-gather.9.cloned.1.call-done), kind=kOutput, calls=%fused_computation.17.clone.1 | convolution fusion | flops 19339935744 | bytes 36175876 | tf_op jit(solution)/shard_map/while/body/eval_jaxpr/dot_general | solution.py:25
  608.5 32.9 %fusion.87 = f32[3072,768]{1,0:T(8,128)} fusion(bf16[4,4096,768]{2,1,0:T(8,128)(2,1)} %get-tuple-element.197, s32[]{:T(128)S(6)} %copy.12, bf16[4096,3072]{1,0:T(8,128)(2,1)} %convolution_convert_fusion.2), kind=kOutput, calls=%fused_computation.20.clone.1 | convolution fusion | flops 19453181952 | bytes 40894468 | tf_op jit(solution)/shard_map/while/body/eval_jaxpr/dot_general | solution.py:36
  641.4 0.0 reduce-scatter.3.cloned.1.call-start
  641.5 57.4 %fusion.84 = bf16[4096,3072]{1,0:T(8,128)(2,1)} fusion(bf16[4096,3072]{1,0:T(8,128)(2,1)} %convolution_convert_fusion.2, bf16[4,4096,768]{2,1,0:T(8,128)(2,1)} %get-tuple-element.197, s32[]{:T(128)S(6)} %copy.12, bf16[1,3072,768]{2,1,0:T(8,128)(2,1)} %all-gather.11.cloned.1.call-done), kind=kOutput, calls=%fused_computation.8.clone.clone.2.clone.1 | convolution fusion | flops 19591593984 | bytes 61341700 | tf_op jit(solution)/shard_map/while/body/eval_jaxpr/dot_general | solution.py:34
  698.9 26.6 %fusion.85 = f32[768,3072]{1,0:T(8,128)} fusion(s32[]{:T(128)S(6)} %copy.12, bf16[4,4096,768]{2,1,0:T(8,128)(2,1)} %get-tuple-element.196, bf16[4096,3072]{1,0:T(8,128)(2,1)} %fusion.84), kind=kOutput, calls=%fused_computation.15.clone.3 | convolution fusion | flops 19327352832 | bytes 40894468 | tf_op jit(solution)/shard_map/while/body/eval_jaxpr/dot_general | solution.py:37
  725.5 36.8 %bitcast_dynamic-update-slice_fusion.2 = bf16[4,4096,768]{2,1,0:T(8,128)(2,1)} fusion(bf16[4,4096,768]{2,1,0:T(8,128)(2,1)} %get-tuple-element.186, s32[]{:T(128)S(6)} %copy.12, bf16[4,4096,768]{2,1,0:T(8,128)(2,1)} %get-tuple-element.196, bf16[1,3072,768]{2,1,0:T(8,128)(2,1)} %all-gather.11.cloned.1.call-done, ...), kind=kOutput, calls=%fused_computation.19.clone.1 | convolution fusion | flops 19462619136 | bytes 42467332 | tf_op jit(solution)/shard_map/while/body/eval_jaxpr/dot_general | solution.py:28
  762.3 1.2 fusion.88
  763.6 41.5 %reduce-scatter.3.cloned.1.call-done = f32[48,3072]{1,0:T(8,128)} async-done(((f32[768,3072]{1,0:T(8,128)}), f32[48,3072]{1,0:T(8,128)}) %reduce-scatter.3.cloned.1.call-update) | async-done | bytes 589840 | tf_op jit(solution)/shard_map/while/body/eval_jaxpr/reduce_scatter | solution.py:39
  805.1 1.2 fusion.86
  806.3 0.8 copy-done.3
  807.1 0.7 all-gather.9.cloned.1.call-update
  807.8 0.0 all-gather.11.cloned.1.call-start
  807.9 0.5 all-gather.11.cloned.1.call-update
  808.4 0.0 reduce-scatter.5.cloned.1.call-start
  808.5 38.4 %all-gather.9.cloned.1.call-done = bf16[1,768,3072]{2,1,0:T(8,128)(2,1)} async-done(((bf16[1,48,3072]{2,1,0:T(8,128)(2,1)}), bf16[1,768,3072]{2,1,0:T(8,128)(2,1)}) %all-gather.9.cloned.1.call-update) | async-done | bytes 4718608 | tf_op jit(solution)/shard_map/while/body/eval_jaxpr/all_gather | solution.py:23
  846.8 26.9 %convolution_convert_fusion.2 = bf16[4096,3072]{1,0:T(8,128)(2,1)} fusion(bf16[4,4096,768]{2,1,0:T(8,128)(2,1)} %get-tuple-element.196, s32[]{:T(128)S(6)} %copy.12, bf16[1,768,3072]{2,1,0:T(8,128)(2,1)} %all-gather.9.cloned.1.call-done), kind=kOutput, calls=%fused_computation.17.clone.1 | convolution fusion | flops 19339935744 | bytes 36175876 | tf_op jit(solution)/shard_map/while/body/eval_jaxpr/dot_general | solution.py:25
  873.7 32.9 %fusion.87 = f32[3072,768]{1,0:T(8,128)} fusion(bf16[4,4096,768]{2,1,0:T(8,128)(2,1)} %get-tuple-element.197, s32[]{:T(128)S(6)} %copy.12, bf16[4096,3072]{1,0:T(8,128)(2,1)} %convolution_convert_fusion.2), kind=kOutput, calls=%fused_computation.20.clone.1 | convolution fusion | flops 19453181952 | bytes 40894468 | tf_op jit(solution)/shard_map/while/body/eval_jaxpr/dot_general | solution.py:36
  906.6 0.0 reduce-scatter.3.cloned.1.call-start
  906.7 57.4 %fusion.84 = bf16[4096,3072]{1,0:T(8,128)(2,1)} fusion(bf16[4096,3072]{1,0:T(8,128)(2,1)} %convolution_convert_fusion.2, bf16[4,4096,768]{2,1,0:T(8,128)(2,1)} %get-tuple-element.197, s32[]{:T(128)S(6)} %copy.12, bf16[1,3072,768]{2,1,0:T(8,128)(2,1)} %all-gather.11.cloned.1.call-done), kind=kOutput, calls=%fused_computation.8.clone.clone.2.clone.1 | convolution fusion | flops 19591593984 | bytes 61341700 | tf_op jit(solution)/shard_map/while/body/eval_jaxpr/dot_general | solution.py:34
  964.1 26.6 %fusion.85 = f32[768,3072]{1,0:T(8,128)} fusion(s32[]{:T(128)S(6)} %copy.12, bf16[4,4096,768]{2,1,0:T(8,128)(2,1)} %get-tuple-element.196, bf16[4096,3072]{1,0:T(8,128)(2,1)} %fusion.84), kind=kOutput, calls=%fused_computation.15.clone.3 | convolution fusion | flops 19327352832 | bytes 40894468 | tf_op jit(solution)/shard_map/while/body/eval_jaxpr/dot_general | solution.py:37
  990.7 36.8 %bitcast_dynamic-update-slice_fusion.2 = bf16[4,4096,768]{2,1,0:T(8,128)(2,1)} fusion(bf16[4,4096,768]{2,1,0:T(8,128)(2,1)} %get-tuple-element.186, s32[]{:T(128)S(6)} %copy.12, bf16[4,4096,768]{2,1,0:T(8,128)(2,1)} %get-tuple-element.196, bf16[1,3072,768]{2,1,0:T(8,128)(2,1)} %all-gather.11.cloned.1.call-done, ...), kind=kOutput, calls=%fused_computation.19.clone.1 | convolution fusion | flops 19462619136 | bytes 42467332 | tf_op jit(solution)/shard_map/while/body/eval_jaxpr/dot_general | solution.py:28
  1027.6 1.2 fusion.88
  1028.8 41.5 %reduce-scatter.3.cloned.1.call-done = f32[48,3072]{1,0:T(8,128)} async-done(((f32[768,3072]{1,0:T(8,128)}), f32[48,3072]{1,0:T(8,128)}) %reduce-scatter.3.cloned.1.call-update) | async-done | bytes 589840 | tf_op jit(solution)/shard_map/while/body/eval_jaxpr/reduce_scatter | solution.py:39
  1070.3 1.2 fusion.86
  1071.5 0.8 copy-done.3
  (48 shorter events, 0.3 us)
Async XLA Ops:
  8.9 42.5 %all-gather.9.cloned.1.call-start = ((), (), s32[]{:S(2)}) async-start(), calls=%async_computation.2 | async-start | bytes 5013504 | tf_op jit(solution)/shard_map/while/body/eval_jaxpr/all_gather | solution.py:23
  9.6 101.7 %all-gather.11.cloned.1.call-start = ((), (), s32[]{:S(2)}) async-start(), calls=%async_computation.3 | async-start | bytes 5013504 | tf_op jit(solution)/shard_map/while/body/eval_jaxpr/all_gather | solution.py:32
  10.4 221.8 %reduce-scatter.5.cloned.1.call-start = ((), (), s32[]{:S(2)}) async-start(), calls=%async_computation.5 | async-start | bytes 10027008 | tf_op jit(solution)/shard_map/while/body/eval_jaxpr/reduce_scatter | solution.py:38
  111.2 163.6 %reduce-scatter.3.cloned.1.call-start = ((), (), s32[]{:S(2)}) async-start(), calls=%async_computation.4 | async-start | bytes 10027008 | tf_op jit(solution)/shard_map/while/body/eval_jaxpr/reduce_scatter | solution.py:39
  195.3 36.8 %copy-start = (f32[1,192,768]{2,1,0:T(8,128)S(1)}, f32[1,192,768]{2,1,0:T(8,128)}, u32[]{:S(2)}) copy-start(f32[1,192,768]{2,1,0:T(8,128)} %get-tuple-element.185) | copy-start | bytes 1769476 | tf_op jit(solution)/shard_map/while
  195.3 79.6 %copy-start.2 = (f32[1,48,3072]{2,1,0:T(8,128)S(1)}, f32[1,48,3072]{2,1,0:T(8,128)}, u32[]{:S(2)}) copy-start(f32[1,48,3072]{2,1,0:T(8,128)} %get-tuple-element.184) | copy-start | bytes 1769476 | tf_op jit(solution)/shard_map/while
  233.3 42.8 %copy-start.1 = (f32[1,192,768]{2,1,0:T(8,128)}, f32[1,192,768]{2,1,0:T(8,128)S(1)}, u32[]{:S(2)}) copy-start(f32[1,192,768]{2,1,0:T(8,128)S(1)} %fusion.88) | copy-start | bytes 1769476 | tf_op jit(solution)/shard_map/while
  276.1 0.8 copy-start.3
  276.9 39.4 %all-gather.9.cloned.1.call-start = ((), (), s32[]{:S(2)}) async-start(), calls=%async_computation.2 | async-start | bytes 5013504 | tf_op jit(solution)/shard_map/while/body/eval_jaxpr/all_gather | solution.py:23
  277.5 98.7 %all-gather.11.cloned.1.call-start = ((), (), s32[]{:S(2)}) async-start(), calls=%async_computation.3 | async-start | bytes 5013504 | tf_op jit(solution)/shard_map/while/body/eval_jaxpr/all_gather | solution.py:32
  278.1 219.0 %reduce-scatter.5.cloned.1.call-start = ((), (), s32[]{:S(2)}) async-start(), calls=%async_computation.5 | async-start | bytes 10027008 | tf_op jit(solution)/shard_map/while/body/eval_jaxpr/reduce_scatter | solution.py:38
  376.2 163.7 %reduce-scatter.3.cloned.1.call-start = ((), (), s32[]{:S(2)}) async-start(), calls=%async_computation.4 | async-start | bytes 10027008 | tf_op jit(solution)/shard_map/while/body/eval_jaxpr/reduce_scatter | solution.py:39
  460.2 36.8 %copy-start = (f32[1,192,768]{2,1,0:T(8,128)S(1)}, f32[1,192,768]{2,1,0:T(8,128)}, u32[]{:S(2)}) copy-start(f32[1,192,768]{2,1,0:T(8,128)} %get-tuple-element.185) | copy-start | bytes 1769476 | tf_op jit(solution)/shard_map/while
  460.2 79.6 %copy-start.2 = (f32[1,48,3072]{2,1,0:T(8,128)S(1)}, f32[1,48,3072]{2,1,0:T(8,128)}, u32[]{:S(2)}) copy-start(f32[1,48,3072]{2,1,0:T(8,128)} %get-tuple-element.184) | copy-start | bytes 1769476 | tf_op jit(solution)/shard_map/while
  498.3 42.8 %copy-start.1 = (f32[1,192,768]{2,1,0:T(8,128)}, f32[1,192,768]{2,1,0:T(8,128)S(1)}, u32[]{:S(2)}) copy-start(f32[1,192,768]{2,1,0:T(8,128)S(1)} %fusion.88) | copy-start | bytes 1769476 | tf_op jit(solution)/shard_map/while
  541.1 0.8 copy-start.3
  541.9 39.7 %all-gather.9.cloned.1.call-start = ((), (), s32[]{:S(2)}) async-start(), calls=%async_computation.2 | async-start | bytes 5013504 | tf_op jit(solution)/shard_map/while/body/eval_jaxpr/all_gather | solution.py:23
  542.6 98.9 %all-gather.11.cloned.1.call-start = ((), (), s32[]{:S(2)}) async-start(), calls=%async_computation.3 | async-start | bytes 5013504 | tf_op jit(solution)/shard_map/while/body/eval_jaxpr/all_gather | solution.py:32
  543.2 219.1 %reduce-scatter.5.cloned.1.call-start = ((), (), s32[]{:S(2)}) async-start(), calls=%async_computation.5 | async-start | bytes 10027008 | tf_op jit(solution)/shard_map/while/body/eval_jaxpr/reduce_scatter | solution.py:38
  641.4 163.6 %reduce-scatter.3.cloned.1.call-start = ((), (), s32[]{:S(2)}) async-start(), calls=%async_computation.4 | async-start | bytes 10027008 | tf_op jit(solution)/shard_map/while/body/eval_jaxpr/reduce_scatter | solution.py:39
  725.5 36.8 %copy-start = (f32[1,192,768]{2,1,0:T(8,128)S(1)}, f32[1,192,768]{2,1,0:T(8,128)}, u32[]{:S(2)}) copy-start(f32[1,192,768]{2,1,0:T(8,128)} %get-tuple-element.185) | copy-start | bytes 1769476 | tf_op jit(solution)/shard_map/while
  725.5 79.6 %copy-start.2 = (f32[1,48,3072]{2,1,0:T(8,128)S(1)}, f32[1,48,3072]{2,1,0:T(8,128)}, u32[]{:S(2)}) copy-start(f32[1,48,3072]{2,1,0:T(8,128)} %get-tuple-element.184) | copy-start | bytes 1769476 | tf_op jit(solution)/shard_map/while
  763.5 42.8 %copy-start.1 = (f32[1,192,768]{2,1,0:T(8,128)}, f32[1,192,768]{2,1,0:T(8,128)S(1)}, u32[]{:S(2)}) copy-start(f32[1,192,768]{2,1,0:T(8,128)S(1)} %fusion.88) | copy-start | bytes 1769476 | tf_op jit(solution)/shard_map/while
  806.3 0.8 copy-start.3
  807.1 39.7 %all-gather.9.cloned.1.call-start = ((), (), s32[]{:S(2)}) async-start(), calls=%async_computation.2 | async-start | bytes 5013504 | tf_op jit(solution)/shard_map/while/body/eval_jaxpr/all_gather | solution.py:23
  807.8 98.9 %all-gather.11.cloned.1.call-start = ((), (), s32[]{:S(2)}) async-start(), calls=%async_computation.3 | async-start | bytes 5013504 | tf_op jit(solution)/shard_map/while/body/eval_jaxpr/all_gather | solution.py:32
  808.4 219.2 %reduce-scatter.5.cloned.1.call-start = ((), (), s32[]{:S(2)}) async-start(), calls=%async_computation.5 | async-start | bytes 10027008 | tf_op jit(solution)/shard_map/while/body/eval_jaxpr/reduce_scatter | solution.py:38
  906.6 163.6 %reduce-scatter.3.cloned.1.call-start = ((), (), s32[]{:S(2)}) async-start(), calls=%async_computation.4 | async-start | bytes 10027008 | tf_op jit(solution)/shard_map/while/body/eval_jaxpr/reduce_scatter | solution.py:39
  990.7 36.8 %copy-start = (f32[1,192,768]{2,1,0:T(8,128)S(1)}, f32[1,192,768]{2,1,0:T(8,128)}, u32[]{:S(2)}) copy-start(f32[1,192,768]{2,1,0:T(8,128)} %get-tuple-element.185) | copy-start | bytes 1769476 | tf_op jit(solution)/shard_map/while
  990.7 79.6 %copy-start.2 = (f32[1,48,3072]{2,1,0:T(8,128)S(1)}, f32[1,48,3072]{2,1,0:T(8,128)}, u32[]{:S(2)}) copy-start(f32[1,48,3072]{2,1,0:T(8,128)} %get-tuple-element.184) | copy-start | bytes 1769476 | tf_op jit(solution)/shard_map/while
  1028.8 42.8 %copy-start.1 = (f32[1,192,768]{2,1,0:T(8,128)}, f32[1,192,768]{2,1,0:T(8,128)S(1)}, u32[]{:S(2)}) copy-start(f32[1,192,768]{2,1,0:T(8,128)S(1)} %fusion.88) | copy-start | bytes 1769476 | tf_op jit(solution)/shard_map/while
  1071.5 0.8 copy-start.3
Sparse Core Ops, SparseCore 0:
  11.9 39.4 all-gather.8
  53.6 36.6 all-gather.10
  111.4 79.4 reduce-scatter.4
  195.4 79.4 reduce-scatter.2
  279.6 36.6 all-gather.8
  318.4 36.6 all-gather.10
  376.3 79.4 reduce-scatter.4
  460.4 79.4 reduce-scatter.2
  544.9 36.6 all-gather.8
  583.7 36.6 all-gather.10
  641.5 79.4 reduce-scatter.4
  725.6 79.4 reduce-scatter.2
  810.1 36.6 all-gather.8
  848.9 36.6 all-gather.10
  906.8 79.4 reduce-scatter.4
  990.8 79.4 reduce-scatter.2
where the time goes:
time: 1080 us
  matrix products  722 us (67%)
  waiting for transfers between devices  327 us (30%)
  between operations  13.7 us (1%)
    dot_general x4, matrix products, micro(): e = jnp.dot(gy, v2.T, preferred_element_type=jnp.float32)  229 us
    reduce_scatter x4, waiting for transfers between devices, micro(): lax.psum_scatter(p1, AX, scatter_dimension=0, tiled=True)  166 us
    all_gather x4, waiting for transfers between devices, micro(): v1 = lax.all_gather(w1[l], AX, axis=0, tiled=True)  156 us
    dot_general x4, matrix products, micro(): jnp.dot(h, v2, preferred_element_type=jnp.float32)  147 us
    dot_general x4, matrix products, micro(): p2 = jnp.dot(h.T, gy, preferred_element_type=jnp.float32)  132 us
    dot_general x4, matrix products, micro(): jnp.dot(cur, v1, preferred_element_type=jnp.float32).astype(jnp.bfloat16)  108 us
    dot_general x4, matrix products, micro(): p1 = jnp.dot(xl.T, da, preferred_element_type=jnp.float32)  106 us
  transfers between devices with their start and end apart: 16, of which 8 were waited for; matrix products, arithmetic and copies ran while one was open for 67% of the time, Pallas kernels for 0%

commit v1 on v0

v1 whole, which is shorter than its diff:
```python
import functools

import jax
import jax.numpy as jnp
from jax import lax
from jax.experimental import pallas as pl
from jax.experimental.pallas import tpu as pltpu
from jax.sharding import PartitionSpec as P

AX = "fsdp"
F32, BF16 = jnp.float32, jnp.bfloat16
C0 = 0.7978845608028654
C1 = 0.044715
VMEM_LIMIT = 66 * 1024 * 1024 - 2 * 1024 * 1024


def _half_cdf(af):
    sq = af * af
    return 0.5 + 0.5 * jnp.tanh(af * (C0 + (C0 * C1) * sq)), sq


def _dot(p, q, dims=((1,), (0,))):
    return lax.dot_general(p, q, (dims, ((), ())), preferred_element_type=F32)


def _fwd_kernel(fw, x_ref, g_ref, w1_ref, a_ref, h_ref, dw2_ref, acc_ref, sem):
    step, steps = pl.program_id(0), pl.num_programs(0)

    @pl.when(step == 0)
    def _():
        acc_ref[...] = jnp.zeros_like(acc_ref)

    for j in range(w1_ref.shape[1] // fw):
        c = pl.ds(j * fw, fw)
        a = _dot(x_ref[...], w1_ref[:, c]).astype(BF16)
        a_ref[:, c] = a
        af = a.astype(F32)
        s, _ = _half_cdf(af)
        h = (af * s).astype(BF16)
        h_ref[:, c] = h
        acc_ref[c, :] += _dot(h, g_ref[...], ((0,), (0,)))

    @pl.when(step == steps - 1)
    def _():
        copy = pltpu.make_async_copy(acc_ref, dw2_ref, sem)
        copy.start()
        copy.wait()


def _fwd(x, g, w1, tm, fw):
    t, d = x.shape
    ff = w1.shape[1]
    return pl.pallas_call(
        functools.partial(_fwd_kernel, fw),
        grid=(t // tm,),
        in_specs=[pl.BlockSpec((tm, d), lambda i: (i, 0)), pl.BlockSpec((tm, d), lambda i: (i, 0)),
                  pl.BlockSpec((d, ff), lambda i: (0, 0), pipeline_mode=pl.Buffered(1))],
        out_specs=[pl.BlockSpec((tm, ff), lambda i: (i, 0)), pl.BlockSpec((tm, ff), lambda i: (i, 0)),
                   pl.BlockSpec(memory_space=pl.ANY)],
        out_shape=[jax.ShapeDtypeStruct((t, ff), BF16), jax.ShapeDtypeStruct((t, ff), BF16),
                   jax.ShapeDtypeStruct((ff, d), F32)],
        scratch_shapes=[pltpu.VMEM((ff, d), F32), pltpu.SemaphoreType.DMA],
        compiler_params=pltpu.CompilerParams(dimension_semantics=("arbitrary",), vmem_limit_bytes=VMEM_LIMIT),
        cost_estimate=pl.CostEstimate(flops=4 * t * d * ff, bytes_accessed=4 * t * (d + ff), transcendentals=t * ff),
        name="fwd",
    )(x, g, w1)


def _bwd_kernel(fw, x_ref, g_ref, a_ref, w2_ref, dw1_ref, acc_ref, xt_ref, sem):
    step, steps = pl.program_id(0), pl.num_programs(0)

    @pl.when(step == 0)
    def _():
        acc_ref[...] = jnp.zeros_like(acc_ref)

    xt_ref[...] = x_ref[...].T
    for j in range(w2_ref.shape[0] // fw):
        c = pl.ds(j * fw, fw)
        e = _dot(g_ref[...], w2_ref[c, :], ((1,), (1,)))
        af = a_ref[:, c].astype(F32)
        s, sq = _half_cdf(af)
        dg = s + (af * s) * (1.0 - s) * ((2 * C0) + (6 * C0 * C1) * sq)
        da = (dg * e).astype(BF16)
        acc_ref[:, c] += _dot(xt_ref[...], da)

    @pl.when(step == steps - 1)
    def _():
        copy = pltpu.make_async_copy(acc_ref, dw1_ref, sem)
        copy.start()
        copy.wait()


def _bwd(x, g, a, w2, tm, fw):
    t, d = x.shape
    ff = w2.shape[0]
    return pl.pallas_call(
        functools.partial(_bwd_kernel, fw),
        grid=(t // tm,),
        in_specs=[pl.BlockSpec((tm, d), lambda i: (i, 0)), pl.BlockSpec((tm, d), lambda i: (i, 0)),
                  pl.BlockSpec((tm, ff), lambda i: (i, 0)),
                  pl.BlockSpec((ff, d), lambda i: (0, 0), pipeline_mode=pl.Buffered(1))],
        out_specs=pl.BlockSpec(memory_space=pl.ANY),
        out_shape=jax.ShapeDtypeStruct((d, ff), F32),
        scratch_shapes=[pltpu.VMEM((d, ff), F32), pltpu.VMEM((d, tm), BF16), pltpu.SemaphoreType.DMA],
        compiler_params=pltpu.CompilerParams(dimension_semantics=("arbitrary",), vmem_limit_bytes=VMEM_LIMIT),
        cost_estimate=pl.CostEstimate(flops=4 * t * d * ff, bytes_accessed=4 * t * d + 2 * t * ff, transcendentals=t * ff),
        name="bwd",
    )(x, g, a, w2)


def _out_kernel(x_ref, h_ref, w2_ref, y_ref):
    y_ref[...] = (x_ref[...].astype(F32) + _dot(h_ref[...], w2_ref[...])).astype(BF16)


def _out(x, h, w2, tm):
    t, d = x.shape
    ff = w2.shape[0]
    return pl.pallas_call(
        _out_kernel,
        grid=(t // tm,),
        in_specs=[pl.BlockSpec((tm, d), lambda i: (i, 0)), pl.BlockSpec((tm, ff), lambda i: (i, 0)),
                  pl.BlockSpec((ff, d), lambda i: (0, 0), pipeline_mode=pl.Buffered(1))],
        out_specs=pl.BlockSpec((tm, d), lambda i: (i, 0)),
        out_shape=jax.ShapeDtypeStruct((t, d), BF16),
        compiler_params=pltpu.CompilerParams(dimension_semantics=("arbitrary",), vmem_limit_bytes=VMEM_LIMIT),
        cost_estimate=pl.CostEstimate(flops=2 * t * d * ff, bytes_accessed=4 * t * d + 2 * t * ff, transcendentals=0),
        name="out",
    )(x, h, w2)


def solution(mesh):
    spec = P(None, AX, None)

    def body(x, g, w1, w2):
        shape, d = x.shape, x.shape[-1]
        xf, gf = x.reshape(-1, d), g.reshape(-1, d)
        v1 = lax.all_gather(w1[0], AX, axis=0, tiled=True)
        v2 = lax.all_gather(w2[0], AX, axis=0, tiled=True)
        a, h, p2 = _fwd(xf, gf, v1, 512, 512)
        d2 = lax.psum_scatter(p2, AX, scatter_dimension=0, tiled=True)
        p1 = _bwd(xf, gf, a, v2, 512, 512)
        d1 = lax.psum_scatter(p1, AX, scatter_dimension=0, tiled=True)
        h, p1 = lax.optimization_barrier((h, p1))
        y = _out(xf, h, v2, 512)
        return y.reshape(shape), d1[None], d2[None]

    return jax.shard_map(body, mesh=mesh, in_specs=(spec, spec, spec, spec),
                         out_specs=(spec, spec, spec), check_vma=False)
```

time: 1080 us -> 599 us (0.55)
  matrix products: 722 us -> 0 us
  Pallas kernels: 0 us -> 543 us
  waiting for transfers between devices: 327 us -> 42.4 us
    dot_general x20 -> x0, matrix products: 722 us -> none  [the longest x4 229 us: micro(): e = jnp.dot(gy, v2.T, preferred_element_type=jnp.float32)]
    pallas_call x0 -> x3, Pallas kernels: none -> 543 us  [the longest x1 236 us: _bwd(): pl.pallas_call(functools.partial(_bwd_kernel, fw), grid=(t // tm,), in_sp...]
    reduce_scatter x8 -> x2, waiting for transfers between devices: 166 us -> 0.01 us  [the longest x1 0.01 us: body(): d2 = lax.psum_scatter(p2, AX, scatter_dimension=0, tiled=True)]
    all_gather x8 -> x2, waiting for transfers between devices: 156 us -> 41 us  [the longest x1 41 us: body(): v1 = lax.all_gather(w1[0], AX, axis=0, tiled=True)]
  transfers between devices with their start and end apart: 16 -> 4, of which waited for: 8 -> 1; matrix products, arithmetic and copies ran while one was open for 67% -> 0% of each run, Pallas kernels for 0% -> 91%
where the time goes in v1:
time: 599 us
  Pallas kernels  543 us (91%)
  waiting for transfers between devices  42.4 us (7%)
  between operations  13.8 us (2%)
    pallas_call x1, Pallas kernels, _bwd(): pl.pallas_call(functools.partial(_bwd_kernel, fw), grid=(t // tm,), in_sp...  236 us
    pallas_call x1, Pallas kernels, _fwd(): pl.pallas_call(functools.partial(_fwd_kernel, fw), grid=(t // tm,), in_sp...  218 us
    pallas_call x1, Pallas kernels, _out(): pl.pallas_call(_out_kernel, grid=(t // tm,), in_specs=[pl.BlockSpec((tm,...  88.8 us
    all_gather x1, waiting for transfers between devices, body(): v1 = lax.all_gather(w1[0], AX, axis=0, tiled=True)  41 us
  transfers between devices with their start and end apart: 4, of which 1 were waited for; matrix products, arithmetic and copies ran while one was open for 0% of the time, Pallas kernels for 91%

profile of v1, /device:TPU:0, one launch (start us, length us, event | category | flops | bytes accessed | tf_op | source)
XLA Modules:
  0.0 599.1 jit_solution(14999081470544477689)
XLA Ops:
  7.2 0.0 all-gather.5.cloned.1.call-start
  7.2 0.7 all-gather.5.cloned.1.call-update
  7.9 0.0 all-gather.7.cloned.1.call-start
  7.9 0.7 all-gather.7.cloned.1.call-update
  8.6 0.0 reduce-scatter.5.cloned.1.call-start
  8.7 41.0 %all-gather.5.cloned.1.call-done = bf16[1,768,3072]{2,1,0:T(8,128)(2,1)} async-done(((bf16[1,48,3072]{2,1,0:T(8,128)(2,1)}), bf16[1,768,3072]{2,1,0:T(8,128)(2,1)}) %all-gather.5.cloned.1.call-update) | async-done | bytes 4718608 | tf_op jit(solution)/shard_map/all_gather | solution.py:137
  49.7 217.7 %fwd.1 = (bf16[16384,3072]{1,0:T(8,128)(2,1)}, bf16[16384,3072]{1,0:T(8,128)(2,1)}, f32[3072,768]{1,0:T(8,128)}) custom-call(bf16[16384,768]{1,0:T(8,128)(2,1)} %bitcast.9, bf16[16384,768]{1,0:T(8,128)(2,1)} %bitcast.7, bf16[768,3072]{1,0:T(8,128)(2,1)} %bitcast.14), custom_call_target="tpu_custom_call" | custom-call | flops 154618822656 | bytes 251658240 | tf_op jit(solution)/shard_map/fwd/pallas_call | solution.py:53
  267.4 0.0 reduce-scatter.5.cloned.1.call-update
  267.4 0.2 reduce-scatter.3.cloned.1.call-start
  267.7 0.0 all-gather.7.cloned.1.call-done
  267.7 236.0 %bwd.1 = f32[768,3072]{1,0:T(8,128)} custom-call(bf16[16384,768]{1,0:T(8,128)(2,1)} %bitcast.10, bf16[16384,768]{1,0:T(8,128)(2,1)} %bitcast.8, bf16[16384,3072]{1,0:T(8,128)(2,1)} %get-tuple-element.8.a_ref, bf16[3072,768]{1,0:T(8,128)(2,1)} %bitcast.12), custom_call_target="tpu_custom_call" | custom-call | flops 154618822656 | bytes 150994944 | tf_op jit(solution)/shard_map/bwd/pallas_call | solution.py:96
  503.7 0.0 reduce-scatter.3.cloned.1.call-update
  503.7 88.8 %out.1 = bf16[16384,768]{1,0:T(8,128)(2,1)} custom-call(bf16[16384,768]{1,0:T(8,128)(2,1)} %bitcast.11, bf16[16384,3072]{1,0:T(8,128)(2,1)} %get-tuple-element.9.h_ref, bf16[3072,768]{1,0:T(8,128)(2,1)} %bitcast.13), custom_call_target="tpu_custom_call" | custom-call | flops 77309411328 | bytes 150994944 | tf_op jit(solution)/shard_map/out/pallas_call | solution.py:118
  592.5 0.0 reduce-scatter.5.cloned.1.call-done
  592.5 0.0 reduce-scatter.3.cloned.1.call-done
Async XLA Ops:
  7.2 42.5 %all-gather.5.cloned.1.call-start = ((), (), s32[]{:S(2)}) async-start(), calls=%async_computation.4 | async-start | bytes 5013504 | tf_op jit(solution)/shard_map/all_gather | solution.py:137
  7.9 259.8 %all-gather.7.cloned.1.call-start = ((), (), s32[]{:S(2)}) async-start(), calls=%async_computation.5 | async-start | bytes 5013504 | tf_op jit(solution)/shard_map/all_gather | solution.py:138
  8.6 583.9 %reduce-scatter.5.cloned.1.call-start = ((), (), s32[]{:S(2)}) async-start(), calls=%async_computation.3 | async-start | bytes 10027008 | tf_op jit(solution)/shard_map/reduce_scatter | solution.py:140
  267.4 325.1 %reduce-scatter.3.cloned.1.call-start = ((), (), s32[]{:S(2)}) async-start(), calls=%async_computation.2 | async-start | bytes 10027008 | tf_op jit(solution)/shard_map/reduce_scatter | solution.py:142
Sparse Core Ops, SparseCore 0:
  10.2 39.4 all-gather.4
  51.9 36.6 all-gather.6
  267.6 79.6 reduce-scatter.4
  503.8 79.6 reduce-scatter.2

commit v2 on v0

v2 whole, which is shorter than its diff:
```python
import functools

import jax
import jax.numpy as jnp
from jax import lax
from jax.experimental import pallas as pl
from jax.experimental.pallas import tpu as pltpu
from jax.sharding import PartitionSpec as P

AX = "fsdp"
F32, BF16 = jnp.float32, jnp.bfloat16
C0 = 0.7978845608028654
C1 = 0.044715
TM = 1024
FW = 256
RB = 256
AB = 64
HEAD = 768
PARAMS = dict(dimension_semantics=("arbitrary",), vmem_limit_bytes=64 * 1024 * 1024 - 65536)


def _half_cdf(af):
    sq = af * af
    return 0.5 + 0.5 * jnp.tanh(af * (C0 + (C0 * C1) * sq)), sq


def _dot(p, q, dims=((1,), (0,))):
    return lax.dot_general(p, q, (dims, ((), ())), preferred_element_type=F32)


def _clear(ref):
    @pl.when(pl.program_id(0) == 0)
    def _():
        @pl.loop(0, ref.shape[0] // 8)
        def _(i):
            ref[pl.ds(pl.multiple_of(i * 8, 8), 8), :] = jnp.zeros((8, ref.shape[1]), F32)


def _flush(src, dst, sem):
    @pl.when(pl.program_id(0) == pl.num_programs(0) - 1)
    def _():
        copy = pltpu.make_async_copy(src, dst, sem)
        copy.start()
        copy.wait()


def _mix(matmuls, others):
    done = 0
    for i, piece in enumerate(matmuls):
        piece()
        while done < len(others) * (i + 1) // len(matmuls):
            others[done]()
            done += 1
    for piece in others[done:]:
        piece()


def _skewed(n, first, act, second, prologue=()):
    for j in range(n + 2):
        matmuls, others = [], list(prologue) if j == 0 else []
        if j < n:
            matmuls += first(j)
        if 0 <= j - 2 < n:
            matmuls += second(j - 2)
        if 0 <= j - 1 < n:
            others += act(j - 1)
        _mix(matmuls, others)


def _fwd_kernel(row0, *refs):
    x_ref, g_ref, w1_ref = refs[:3]
    a_ref, h_ref, dw2_ref, acc_ref, sem = refs[-5:]
    tm, ff = x_ref.shape[0], w1_ref.shape[1]
    _clear(acc_ref)

    def first(j):
        c = pl.ds(j * FW, FW)

        def piece(r):
            q = pl.ds(r * RB, RB)
            a_ref[q, c] = _dot(x_ref[q, :], w1_ref[:, c]).astype(BF16)

        return [functools.partial(piece, r) for r in range(tm // RB)]

    def act(j):
        c = pl.ds(j * FW, FW)

        def piece(r):
            q = pl.ds(r * AB, AB)
            af = a_ref[q, c].astype(F32)
            s, _ = _half_cdf(af)
            h_ref[q, c] = (af * s).astype(BF16)

        return [functools.partial(piece, r) for r in range(tm // AB)]

    def second(j):
        c = pl.ds(j * FW, FW)

        def piece():
            acc_ref[c, :] += _dot(h_ref[:, c], g_ref[...], ((0,), (0,)))

        return [piece]

    _skewed(ff // FW, first, act, second)
    _flush(acc_ref, dw2_ref.at[pl.ds(row0, ff), :], sem)


def _fwd(x, g, w1, row0, rows, dw2=None):
    (t, d), ff = x.shape, w1.shape[1]
    token = lambda n: pl.BlockSpec((TM, n), lambda i: (i, 0))
    hbm = pl.BlockSpec(memory_space=pl.ANY)
    more = [] if dw2 is None else [dw2]
    return pl.pallas_call(
        functools.partial(_fwd_kernel, row0),
        grid=(t // TM,),
        in_specs=[token(d), token(d), pl.BlockSpec((d, ff), lambda i: (0, 0), pipeline_mode=pl.Buffered(1))]
        + [hbm] * len(more),
        out_specs=[token(ff), token(ff), hbm],
        out_shape=[jax.ShapeDtypeStruct((t, ff), BF16), jax.ShapeDtypeStruct((t, ff), BF16),
                   jax.ShapeDtypeStruct((rows, d), F32)],
        scratch_shapes=[pltpu.VMEM((ff, d), F32), pltpu.SemaphoreType.DMA],
        input_output_aliases={3: 2} if more else {},
        compiler_params=pltpu.CompilerParams(**PARAMS),
        cost_estimate=pl.CostEstimate(flops=4 * t * d * ff, bytes_accessed=4 * t * (d + ff), transcendentals=t * ff),
        name="fwd",
    )(x, g, w1, *more)


def _bwd_kernel(x_ref, g_ref, a0_ref, a1_ref, w2_ref, dw1_ref, acc_ref, xt_ref, sem, e0, e1, b0, b1):
    tm, ff, head = x_ref.shape[0], w2_ref.shape[0], a0_ref.shape[1]
    es, das = (e0, e1), (b0, b1)
    _clear(acc_ref)

    def first(j):
        c = pl.ds(j * FW, FW)

        def piece(r):
            q = pl.ds(r * RB, RB)
            es[j % 2][q, :] = _dot(g_ref[q, :], w2_ref[c, :], ((1,), (1,)))

        return [functools.partial(piece, r) for r in range(tm // RB)]

    def act(j):
        col = j * FW
        a_ref, col = (a0_ref, col) if col < head else (a1_ref, col - head)

        def piece(r):
            q = pl.ds(r * AB, AB)
            af = a_ref[q, pl.ds(col, FW)].astype(F32)
            s, sq = _half_cdf(af)
            slope = s + (s * (1.0 - s)) * (af * ((2 * C0) + (6 * C0 * C1) * sq))
            das[j % 2][q, :] = (slope * es[j % 2][q, :]).astype(BF16)

        return [functools.partial(piece, r) for r in range(tm // AB)]

    def second(j):
        c = pl.ds(j * FW, FW)

        def piece():
            acc_ref[:, c] += _dot(xt_ref[...], das[j % 2][...])

        return [piece]

    def transpose(r):
        q = pl.ds(r * 128, 128)
        xt_ref[:, q] = x_ref[q, :].T

    _skewed(ff // FW, first, act, second, [functools.partial(transpose, r) for r in range(tm // 128)])
    _flush(acc_ref, dw1_ref, sem)


def _bwd(x, g, a0, a1, w2):
    (t, d), ff = x.shape, w2.shape[0]
    token = lambda n: pl.BlockSpec((TM, n), lambda i: (i, 0))
    return pl.pallas_call(
        _bwd_kernel,
        grid=(t // TM,),
        in_specs=[token(d), token(d), token(a0.shape[1]), token(a1.shape[1]),
                  pl.BlockSpec((ff, d), lambda i: (0, 0), pipeline_mode=pl.Buffered(1))],
        out_specs=pl.BlockSpec(memory_space=pl.ANY),
        out_shape=jax.ShapeDtypeStruct((d, ff), F32),
        scratch_shapes=[pltpu.VMEM((d, ff), F32), pltpu.VMEM((d, TM), BF16), pltpu.SemaphoreType.DMA]
        + [pltpu.VMEM((TM, FW), F32)] * 2 + [pltpu.VMEM((TM, FW), BF16)] * 2,
        compiler_params=pltpu.CompilerParams(**PARAMS),
        cost_estimate=pl.CostEstimate(flops=4 * t * d * ff, bytes_accessed=4 * t * d + 2 * t * ff, transcendentals=t * ff),
        name="bwd",
    )(x, g, a0, a1, w2)


def _out_kernel(x_ref, h0_ref, h1_ref, w2_ref, y_ref):
    head = h0_ref.shape[1]
    for r in range(x_ref.shape[0] // RB):
        q = pl.ds(r * RB, RB)
        z = _dot(h0_ref[q, :], w2_ref[:head, :]) + _dot(h1_ref[q, :], w2_ref[head:, :])
        y_ref[q, :] = (x_ref[q, :].astype(F32) + z).astype(BF16)


def _out(x, h0, h1, w2):
    (t, d), ff = x.shape, w2.shape[0]
    token = lambda n: pl.BlockSpec((TM, n), lambda i: (i, 0))
    return pl.pallas_call(
        _out_kernel,
        grid=(t // TM,),
        in_specs=[token(d), token(h0.shape[1]), token(h1.shape[1]),
                  pl.BlockSpec((ff, d), lambda i: (0, 0), pipeline_mode=pl.Buffered(1))],
        out_specs=token(d),
        out_shape=jax.ShapeDtypeStruct((t, d), BF16),
        compiler_params=pltpu.CompilerParams(**PARAMS),
        cost_estimate=pl.CostEstimate(flops=2 * t * d * ff, bytes_accessed=4 * t * d + 2 * t * ff, transcendentals=0),
        name="out",
    )(x, h0, h1, w2)


def solution(mesh):
    spec = P(None, AX, None)

    def body(x, g, w1, w2):
        shape, d = x.shape, x.shape[-1]
        xf, gf = x.reshape(-1, d), g.reshape(-1, d)
        gather = functools.partial(lax.all_gather, axis_name=AX, axis=0, tiled=True)
        scatter = functools.partial(lax.psum_scatter, axis_name=AX, scatter_dimension=0, tiled=True)
        v1a, v1b = gather(w1[0, :, :HEAD]), gather(w1[0, :, HEAD:])
        v2 = gather(w2[0])
        rows = v2.shape[0]
        a0, h0, p2 = _fwd(xf, gf, v1a, 0, rows)
        a1, h1, p2 = _fwd(xf, gf, v1b, HEAD, rows, p2)
        d2 = scatter(p2)
        p1 = _bwd(xf, gf, a0, a1, v2)
        d1 = scatter(p1)
        h0, h1, p1 = lax.optimization_barrier((h0, h1, p1))
        y = _out(xf, h0, h1, v2)
        return y.reshape(shape), d1[None], d2[None]

    return jax.shard_map(body, mesh=mesh, in_specs=(spec, spec, spec, spec),
                         out_specs=(spec, spec, spec), check_vma=False)
```

time: 1080 us -> 509 us (0.47)
  matrix products: 722 us -> 0 us
  Pallas kernels: 0 us -> 462 us
  waiting for transfers between devices: 327 us -> 28.8 us
    dot_general x20 -> x0, matrix products: 722 us -> none  [the longest x4 229 us: micro(): e = jnp.dot(gy, v2.T, preferred_element_type=jnp.float32)]
    pallas_call x0 -> x4, Pallas kernels: none -> 462 us  [the longest x1 188 us: _bwd(): pl.pallas_call(_bwd_kernel, grid=(t // TM,), in_specs=[token(d), token(d)...]
    reduce_scatter x8 -> x2, waiting for transfers between devices: 166 us -> 0.01 us  [the longest x1 0.01 us: body(): d2 = scatter(p2)]
    all_gather x8 -> x3, waiting for transfers between devices: 156 us -> 28.1 us  [the longest x2 28 us: body(): v1a, v1b = (gather(w1[0, :, :HEAD]), gather(w1[0, :, HEAD:]))]
  transfers between devices with their start and end apart: 16 -> 5, of which waited for: 8 -> 1; matrix products, arithmetic and copies ran while one was open for 67% -> 0% of each run, Pallas kernels for 0% -> 91%
where the time goes in v2:
time: 509 us
  Pallas kernels  462 us (91%)
  waiting for transfers between devices  28.8 us (6%)
  between operations  13.8 us (3%)
    pallas_call x1, Pallas kernels, _bwd(): pl.pallas_call(_bwd_kernel, grid=(t // TM,), in_specs=[token(d), token(d)...  188 us
    pallas_call x2, Pallas kernels, _fwd(): pl.pallas_call(functools.partial(_fwd_kernel, row0), grid=(t // TM,), in_...  187 us
    pallas_call x1, Pallas kernels, _out(): pl.pallas_call(_out_kernel, grid=(t // TM,), in_specs=[token(d), token(h0...  87.9 us
    all_gather x2, waiting for transfers between devices, body(): v1a, v1b = (gather(w1[0, :, :HEAD]), gather(w1[0, :, HEAD:]))  28 us
  transfers between devices with their start and end apart: 5, of which 1 were waited for; matrix products, arithmetic and copies ran while one was open for 0% of the time, Pallas kernels for 91%

profile of v2, /device:TPU:0, one launch (start us, length us, event | category | flops | bytes accessed | tf_op | source)
XLA Modules:
  0.0 508.6 jit_solution(7819089768370643446)
XLA Ops:
  7.2 0.0 all-gather.7.cloned.1.call-start
  7.2 1.5 slice.6
  8.7 0.0 all-gather.7.cloned.1.call-update
  8.8 0.0 all-gather.9.cloned.1.call-start
  8.8 1.6 slice.7
  10.4 0.0 all-gather.9.cloned.1.call-update
  10.5 0.0 all-gather.11.cloned.1.call-start
  10.5 0.7 all-gather.11.cloned.1.call-update
  11.2 0.0 reduce-scatter.5.cloned.1.call-start
  11.3 28.0 %all-gather.7.cloned.1.call-done = bf16[1,768,768]{2,1,0:T(8,128)(2,1)} async-done(((bf16[1,48,768]{2,1,0:T(8,128)(2,1)}), bf16[1,768,768]{2,1,0:T(8,128)(2,1)}) %all-gather.7.cloned.1.call-update) | async-done | bytes 1179664 | tf_op jit(solution)/shard_map/all_gather | solution.py:222
  39.3 51.4 %fwd.2 = (bf16[16384,768]{1,0:T(8,128)(2,1)}, bf16[16384,768]{1,0:T(8,128)(2,1)}, f32[3072,768]{1,0:T(8,128)}) custom-call(bf16[16384,768]{1,0:T(8,128)(2,1)} %bitcast.11, bf16[16384,768]{1,0:T(8,128)(2,1)} %bitcast.8, bf16[768,768]{1,0:T(8,128)(2,1)} %bitcast.18), custom_call_target="tpu_custom_call" | custom-call | flops 38654705664 | bytes 100663296 | tf_op jit(solution)/shard_map/fwd/pallas_call | solution.py:113
  90.7 0.0 all-gather.9.cloned.1.call-done
  90.8 135.5 %fwd.3 = (bf16[16384,2304]{1,0:T(8,128)(2,1)}, bf16[16384,2304]{1,0:T(8,128)(2,1)}, f32[3072,768]{1,0:T(8,128)}) custom-call(bf16[16384,768]{1,0:T(8,128)(2,1)} %bitcast.12, bf16[16384,768]{1,0:T(8,128)(2,1)} %bitcast.9, bf16[768,2304]{1,0:T(8,128)(2,1)} %bitcast.17, f32[3072,768]{1,0:T(8,128)} %get-tuple-element.12.refs_3_), custom_call_target="tpu_custom_call", output_to_operand_aliasing={{2}: (3, {})} | custom-call | flops 115964116992 | bytes 201326592 | tf_op jit(solution)/shard_map/fwd/pallas_call | solution.py:113
  226.3 0.0 reduce-scatter.5.cloned.1.call-update
  226.3 0.2 reduce-scatter.3.cloned.1.call-start
  226.5 0.0 all-gather.11.cloned.1.call-done
  226.6 187.5 %bwd.1 = f32[768,3072]{1,0:T(8,128)} custom-call(bf16[16384,768]{1,0:T(8,128)(2,1)} %bitcast.13, bf16[16384,768]{1,0:T(8,128)(2,1)} %bitcast.10, bf16[16384,768]{1,0:T(8,128)(2,1)} %get-tuple-element.14.a0_ref, bf16[16384,2304]{1,0:T(8,128)(2,1)} %get-tuple-element.15.a1_ref, bf16[3072,768]{1,0:T(8,128)(2,1)} %bitcast.15), custom_call_target="tpu_custom_call" | custom-call | flops 154618822656 | bytes 150994944 | tf_op jit(solution)/shard_map/bwd/pallas_call | solution.py:175
  414.1 0.0 reduce-scatter.3.cloned.1.call-update
  414.1 87.9 %out.1 = bf16[16384,768]{1,0:T(8,128)(2,1)} custom-call(bf16[16384,768]{1,0:T(8,128)(2,1)} %bitcast.14, bf16[16384,768]{1,0:T(8,128)(2,1)} %get-tuple-element.16.h0_ref, bf16[16384,2304]{1,0:T(8,128)(2,1)} %get-tuple-element.17.h1_ref, bf16[3072,768]{1,0:T(8,128)(2,1)} %bitcast.16), custom_call_target="tpu_custom_call" | custom-call | flops 77309411328 | bytes 150994944 | tf_op jit(solution)/shard_map/out/pallas_call | solution.py:201
  502.0 0.0 reduce-scatter.5.cloned.1.call-done
  502.0 0.0 reduce-scatter.3.cloned.1.call-done
Async XLA Ops:
  7.2 32.1 %all-gather.7.cloned.1.call-start = ((), (), s32[]{:S(2)}) async-start(), calls=%async_computation.4 | async-start | bytes 1253376 | tf_op jit(solution)/shard_map/all_gather | solution.py:222
  8.8 82.0 %all-gather.9.cloned.1.call-start = ((), (), s32[]{:S(2)}) async-start(), calls=%async_computation.5 | async-start | bytes 3760128 | tf_op jit(solution)/shard_map/all_gather | solution.py:222
  10.5 216.1 %all-gather.11.cloned.1.call-start = ((), (), s32[]{:S(2)}) async-start(), calls=%async_computation.6 | async-start | bytes 5013504 | tf_op jit(solution)/shard_map/all_gather | solution.py:223
  11.2 490.8 %reduce-scatter.5.cloned.1.call-start = ((), (), s32[]{:S(2)}) async-start(), calls=%async_computation.3 | async-start | bytes 10027008 | tf_op jit(solution)/shard_map/reduce_scatter | solution.py:227
  226.3 275.7 %reduce-scatter.3.cloned.1.call-start = ((), (), s32[]{:S(2)}) async-start(), calls=%async_computation.2 | async-start | bytes 10027008 | tf_op jit(solution)/shard_map/reduce_scatter | solution.py:229
Sparse Core Ops, SparseCore 0:
  10.8 28.4 all-gather.6
  42.1 32.7 all-gather.8
  77.1 36.6 all-gather.10
  226.4 79.4 reduce-scatter.4
  414.2 79.4 reduce-scatter.2

commit v3 on v2

--- a/solution.py
+++ b/solution.py
@@ -15,6 +15,7 @@
 FW = 256
 RB = 256
 AB = 64
+DEVICES = 16
 HEAD = 768
 PARAMS = dict(dimension_semantics=("arbitrary",), vmem_limit_bytes=64 * 1024 * 1024 - 65536)
 
@@ -31,9 +32,11 @@
 def _clear(ref):
     @pl.when(pl.program_id(0) == 0)
     def _():
-        @pl.loop(0, ref.shape[0] // 8)
+        rows = 16
+
+        @pl.loop(0, ref.shape[0] // rows)
         def _(i):
-            ref[pl.ds(pl.multiple_of(i * 8, 8), 8), :] = jnp.zeros((8, ref.shape[1]), F32)
+            ref[pl.ds(pl.multiple_of(i * rows, rows), rows), :] = jnp.zeros((rows, ref.shape[1]), ref.dtype)
 
 
 def _flush(src, dst, sem):
@@ -42,6 +45,50 @@
         copy = pltpu.make_async_copy(src, dst, sem)
         copy.start()
         copy.wait()
+
+
+def _gather_kernel(w_ref, out_ref, send, recv, pass_send, pass_recv):
+    me = lax.axis_index(AX)
+    flip = lambda b: 2**b * (1 - 2 * (me // 2**b % 2))
+    other = me + flip(0)
+    hops = (1, 2, 4, 3, 5, 6, 7)
+    peers = {k: me + sum(flip(b + 1) for b in range(3) if k >> b & 1) for k in hops}
+
+    barrier = pltpu.get_barrier_semaphore()
+    for device in (other, *peers.values()):
+        pl.semaphore_signal(barrier, inc=1, device_id=(device,), device_id_type=pl.DeviceIdType.MESH)
+    pl.semaphore_wait(barrier, 1 + len(hops))
+
+    def push(src, block, device, s, r):
+        copy = pltpu.make_async_remote_copy(src_ref=src, dst_ref=out_ref.at[block], send_sem=s, recv_sem=r,
+                                            device_id=(device,), device_id_type=pl.DeviceIdType.MESH)
+        copy.start()
+        return copy
+
+    own = w_ref.at[0, :, pl.ds(0, out_ref.shape[2])]
+    direct = {k: push(own, me, peers[k], send.at[k], recv.at[k]) for k in hops}
+    passed = [push(own, me, other, pass_send.at[0], pass_recv.at[0])]
+    out_ref[me] = own[...]
+    for k in hops:
+        direct[k].wait_recv()
+        passed.append(push(out_ref.at[peers[k]], peers[k], other, pass_send.at[k], pass_recv.at[k]))
+    for copy in passed:
+        copy.wait_recv()
+    for copy in (*direct.values(), *passed):
+        copy.wait_send()
+
+
+def _gather(w1, columns):
+    rows = w1.shape[1]
+    return pl.pallas_call(
+        _gather_kernel,
+        in_specs=[pl.BlockSpec(memory_space=pltpu.VMEM)],
+        out_specs=pl.BlockSpec(memory_space=pltpu.VMEM),
+        out_shape=jax.ShapeDtypeStruct((DEVICES, rows, columns), w1.dtype),
+        scratch_shapes=[pltpu.SemaphoreType.DMA((8,))] * 4,
+        compiler_params=pltpu.CompilerParams(collective_id=0, has_side_effects=True),
+        name="gather",
+    )(w1).reshape(DEVICES * rows, columns)
 
 
 def _mix(matmuls, others):
@@ -67,10 +114,10 @@
         _mix(matmuls, others)
 
 
-def _fwd_kernel(row0, *refs):
+def _fwd_kernel(row0, col0, *refs):
     x_ref, g_ref, w1_ref = refs[:3]
     a_ref, h_ref, dw2_ref, acc_ref, sem = refs[-5:]
-    tm, ff = x_ref.shape[0], w1_ref.shape[1]
+    tm, ff = a_ref.shape
     _clear(acc_ref)
 
     def first(j):
@@ -78,7 +125,7 @@
 
         def piece(r):
             q = pl.ds(r * RB, RB)
-            a_ref[q, c] = _dot(x_ref[q, :], w1_ref[:, c]).astype(BF16)
+            a_ref[q, c] = _dot(x_ref[q, :], w1_ref[:, pl.ds(col0 + j * FW, FW)]).astype(BF16)
 
         return [functools.partial(piece, r) for r in range(tm // RB)]
 
@@ -105,15 +152,15 @@
     _flush(acc_ref, dw2_ref.at[pl.ds(row0, ff), :], sem)
 
 
-def _fwd(x, g, w1, row0, rows, dw2=None):
-    (t, d), ff = x.shape, w1.shape[1]
-    token = lambda n: pl.BlockSpec((TM, n), lambda i: (i, 0))
+def _fwd(x, g, w1, col0, row0, rows, tm, dw2=None):
+    (t, d), ff = x.shape, w1.shape[1] - col0
+    token = lambda n: pl.BlockSpec((tm, n), lambda i: (i, 0))
     hbm = pl.BlockSpec(memory_space=pl.ANY)
     more = [] if dw2 is None else [dw2]
     return pl.pallas_call(
-        functools.partial(_fwd_kernel, row0),
-        grid=(t // TM,),
-        in_specs=[token(d), token(d), pl.BlockSpec((d, ff), lambda i: (0, 0), pipeline_mode=pl.Buffered(1))]
+        functools.partial(_fwd_kernel, row0, col0),
+        grid=(t // tm,),
+        in_specs=[token(d), token(d), pl.BlockSpec(w1.shape, lambda i: (0, 0), pipeline_mode=pl.Buffered(1))]
         + [hbm] * len(more),
         out_specs=[token(ff), token(ff), hbm],
         out_shape=[jax.ShapeDtypeStruct((t, ff), BF16), jax.ShapeDtypeStruct((t, ff), BF16),
@@ -219,11 +266,12 @@
         xf, gf = x.reshape(-1, d), g.reshape(-1, d)
         gather = functools.partial(lax.all_gather, axis_name=AX, axis=0, tiled=True)
         scatter = functools.partial(lax.psum_scatter, axis_name=AX, scatter_dimension=0, tiled=True)
-        v1a, v1b = gather(w1[0, :, :HEAD]), gather(w1[0, :, HEAD:])
-        v2 = gather(w2[0])
+        v1a = _gather(w1, HEAD)
+        v1a, w1b, w2 = lax.optimization_barrier((v1a, w1[0, :, HEAD:], w2))
+        v1b, v2 = gather(w1b), gather(w2[0])
         rows = v2.shape[0]
-        a0, h0, p2 = _fwd(xf, gf, v1a, 0, rows)
-        a1, h1, p2 = _fwd(xf, gf, v1b, HEAD, rows, p2)
+        a0, h0, p2 = _fwd(xf, gf, v1a, 0, 0, rows, 2 * TM)
+        a1, h1, p2 = _fwd(xf, gf, v1b, 0, HEAD, rows, TM, p2)
         d2 = scatter(p2)
         p1 = _bwd(xf, gf, a0, a1, v2)
         d1 = scatter(p1)

time: 509 us -> 493 us (0.969)
  waiting for transfers between devices: 28.8 us -> 0.79 us
  Pallas kernels: 462 us -> 476 us
    all_gather x3 -> x2, waiting for transfers between devices: 28.1 us -> 0.04 us  [body(): v1b, v2 = (gather(w1b), gather(w2[0]))]
    pallas_call x2 -> x3, Pallas kernels: 187 us -> 201 us  [the longest x2 184 us: _fwd(): pl.pallas_call(functools.partial(_fwd_kernel, row0, col0), grid=(t // tm,...]
  transfers between devices with their start and end apart: 5 -> 4, of which waited for: 1 -> 0; matrix products, arithmetic and copies ran while one was open for 0% -> 0% of each run, Pallas kernels for 91% -> 93%
where the time goes in v3:
time: 493 us
  Pallas kernels  476 us (97%)
  between operations  13.8 us (3%)
    pallas_call x1, Pallas kernels, _bwd(): pl.pallas_call(_bwd_kernel, grid=(t // TM,), in_specs=[token(d), token(d)...  187 us
    pallas_call x2, Pallas kernels, _fwd(): pl.pallas_call(functools.partial(_fwd_kernel, row0, col0), grid=(t // tm,...  184 us
    pallas_call x1, Pallas kernels, _out(): pl.pallas_call(_out_kernel, grid=(t // TM,), in_specs=[token(d), token(h0...  87.9 us
    pallas_call x1, Pallas kernels, _gather(): pl.pallas_call(_gather_kernel, in_specs=[pl.BlockSpec(memory_space=pltpu....  16.4 us
  transfers between devices with their start and end apart: 4, of which 0 were waited for; matrix products, arithmetic and copies ran while one was open for 0% of the time, Pallas kernels for 93%

profile of v3, /device:TPU:0, one launch (start us, length us, event | category | flops | bytes accessed | tf_op | source)
XLA Modules:
  0.0 492.5 jit_solution(13302621249409047998)
XLA Ops:
  7.2 0.0 all-gather.4.cloned.1.call-start
  7.2 16.4 %gather.1 = bf16[16,48,768]{2,1,0:T(8,128)(2,1)} custom-call(bf16[1,48,3072]{2,1,0:T(8,128)(2,1)} %w_ref.1), custom_call_target="tpu_custom_call" | custom-call | tf_op jit(solution)/shard_map/gather/pallas_call | solution.py:83
  23.6 1.6 slice_bitcast_fusion
  25.3 0.0 all-gather.4.cloned.1.call-update
  25.3 0.0 all-gather.6.cloned.1.call-start
  25.4 0.7 all-gather.6.cloned.1.call-update
  26.1 0.0 reduce-scatter.5.cloned.1.call-start
  26.1 49.4 %fwd.2 = (bf16[16384,768]{1,0:T(8,128)(2,1)}, bf16[16384,768]{1,0:T(8,128)(2,1)}, f32[3072,768]{1,0:T(8,128)}) custom-call(bf16[16384,768]{1,0:T(8,128)(2,1)} %bitcast.13, bf16[16384,768]{1,0:T(8,128)(2,1)} %bitcast.10, bf16[768,768]{1,0:T(8,128)(2,1)} %bitcast.9), custom_call_target="tpu_custom_call" | custom-call | flops 38654705664 | bytes 100663296 | tf_op jit(solution)/shard_map/fwd/pallas_call | solution.py:160
  75.5 0.0 all-gather.4.cloned.1.call-done.refs_2_
  75.5 134.9 %fwd.3 = (bf16[16384,2304]{1,0:T(8,128)(2,1)}, bf16[16384,2304]{1,0:T(8,128)(2,1)}, f32[3072,768]{1,0:T(8,128)}) custom-call(bf16[16384,768]{1,0:T(8,128)(2,1)} %bitcast.14, bf16[16384,768]{1,0:T(8,128)(2,1)} %bitcast.11, bf16[768,2304]{1,0:T(8,128)(2,1)} %all-gather.4.cloned.1.call-done.refs_2_, ...), custom_call_target="tpu_custom_call", output_to_operand_aliasing={{2}: (3, {})} | custom-call | flops 115964116992 | bytes 201326592 | tf_op jit(solution)/shard_map/fwd/pallas_call | solution.py:160
  210.4 0.0 reduce-scatter.5.cloned.1.call-update
  210.4 0.2 reduce-scatter.3.cloned.1.call-start
  210.6 0.0 all-gather.6.cloned.1.call-done
  210.7 187.4 %bwd.1 = f32[768,3072]{1,0:T(8,128)} custom-call(bf16[16384,768]{1,0:T(8,128)(2,1)} %bitcast.15, bf16[16384,768]{1,0:T(8,128)(2,1)} %bitcast.12, bf16[16384,768]{1,0:T(8,128)(2,1)} %get-tuple-element.19.a0_ref, bf16[16384,2304]{1,0:T(8,128)(2,1)} %get-tuple-element.20.a1_ref, bf16[3072,768]{1,0:T(8,128)(2,1)} %bitcast.17), custom_call_target="tpu_custom_call" | custom-call | flops 154618822656 | bytes 150994944 | tf_op jit(solution)/shard_map/bwd/pallas_call | solution.py:222
  398.0 0.0 reduce-scatter.3.cloned.1.call-update
  398.1 87.9 %out.1 = bf16[16384,768]{1,0:T(8,128)(2,1)} custom-call(bf16[16384,768]{1,0:T(8,128)(2,1)} %bitcast.16, bf16[16384,768]{1,0:T(8,128)(2,1)} %get-tuple-element.22.h0_ref, bf16[16384,2304]{1,0:T(8,128)(2,1)} %get-tuple-element.23.h1_ref, bf16[3072,768]{1,0:T(8,128)(2,1)} %bitcast.18), custom_call_target="tpu_custom_call" | custom-call | flops 77309411328 | bytes 150994944 | tf_op jit(solution)/shard_map/out/pallas_call | solution.py:248
  486.0 0.0 reduce-scatter.5.cloned.1.call-done
  486.0 0.0 reduce-scatter.3.cloned.1.call-done
Async XLA Ops:
  7.2 68.4 %all-gather.4.cloned.1.call-start = ((), (), s32[]{:S(2)}) async-start(), calls=%async_computation.2 | async-start | bytes 3760128 | tf_op jit(solution)/shard_map/all_gather | solution.py:271
  25.3 185.4 %all-gather.6.cloned.1.call-start = ((), (), s32[]{:S(2)}) async-start(), calls=%async_computation.5 | async-start | bytes 5013504 | tf_op jit(solution)/shard_map/all_gather | solution.py:271
  26.1 459.9 %reduce-scatter.5.cloned.1.call-start = ((), (), s32[]{:S(2)}) async-start(), calls=%async_computation.4 | async-start | bytes 10027008 | tf_op jit(solution)/shard_map/reduce_scatter | solution.py:275
  210.4 275.6 %reduce-scatter.3.cloned.1.call-start = ((), (), s32[]{:S(2)}) async-start(), calls=%async_computation.3 | async-start | bytes 10027008 | tf_op jit(solution)/shard_map/reduce_scatter | solution.py:277
Sparse Core Ops, SparseCore 0:
  25.4 33.0 all-gather.3
  60.7 36.6 all-gather.5
  210.5 79.6 reduce-scatter.4
  398.2 79.7 reduce-scatter.2

commit v4 on v3

--- a/solution.py
+++ b/solution.py
@@ -47,7 +47,7 @@
         copy.wait()
 
 
-def _gather_kernel(w_ref, out_ref, send, recv, pass_send, pass_recv):
+def _gather_kernel(w_ref, out_ref, rest_ref, send, recv, pass_send, pass_recv):
     me = lax.axis_index(AX)
     flip = lambda b: 2**b * (1 - 2 * (me // 2**b % 2))
     other = me + flip(0)
@@ -69,6 +69,7 @@
     direct = {k: push(own, me, peers[k], send.at[k], recv.at[k]) for k in hops}
     passed = [push(own, me, other, pass_send.at[0], pass_recv.at[0])]
     out_ref[me] = own[...]
+    rest_ref[...] = w_ref[:, :, out_ref.shape[2]:]
     for k in hops:
         direct[k].wait_recv()
         passed.append(push(out_ref.at[peers[k]], peers[k], other, pass_send.at[k], pass_recv.at[k]))
@@ -79,16 +80,19 @@
 
 
 def _gather(w1, columns):
-    rows = w1.shape[1]
-    return pl.pallas_call(
+    _, rows, ff = w1.shape
+    vmem = pl.BlockSpec(memory_space=pltpu.VMEM)
+    whole, rest = pl.pallas_call(
         _gather_kernel,
-        in_specs=[pl.BlockSpec(memory_space=pltpu.VMEM)],
-        out_specs=pl.BlockSpec(memory_space=pltpu.VMEM),
-        out_shape=jax.ShapeDtypeStruct((DEVICES, rows, columns), w1.dtype),
+        in_specs=[vmem],
+        out_specs=[vmem, vmem],
+        out_shape=[jax.ShapeDtypeStruct((DEVICES, rows, columns), w1.dtype),
+                   jax.ShapeDtypeStruct((1, rows, ff - columns), w1.dtype)],
         scratch_shapes=[pltpu.SemaphoreType.DMA((8,))] * 4,
         compiler_params=pltpu.CompilerParams(collective_id=0, has_side_effects=True),
         name="gather",
-    )(w1).reshape(DEVICES * rows, columns)
+    )(w1)
+    return whole.reshape(DEVICES * rows, columns), rest
 
 
 def _mix(matmuls, others):
@@ -102,13 +106,11 @@
         piece()
 
 
-def _skewed(n, first, act, second, prologue=()):
+def _skewed(n, first, act, second, prologue=(), second_leads=False):
     for j in range(n + 2):
-        matmuls, others = [], list(prologue) if j == 0 else []
-        if j < n:
-            matmuls += first(j)
-        if 0 <= j - 2 < n:
-            matmuls += second(j - 2)
+        ahead, others = first(j) if j < n else [], list(prologue) if j == 0 else []
+        behind = second(j - 2) if 0 <= j - 2 < n else []
+        matmuls = behind + ahead if second_leads else ahead + behind
         if 0 <= j - 1 < n:
             others += act(j - 1)
         _mix(matmuls, others)
@@ -182,10 +184,10 @@
         c = pl.ds(j * FW, FW)
 
         def piece(r):
-            q = pl.ds(r * RB, RB)
+            q = pl.ds(r * 2 * RB, 2 * RB)
             es[j % 2][q, :] = _dot(g_ref[q, :], w2_ref[c, :], ((1,), (1,)))
 
-        return [functools.partial(piece, r) for r in range(tm // RB)]
+        return [functools.partial(piece, r) for r in range(tm // (2 * RB))]
 
     def act(j):
         col = j * FW
@@ -212,7 +214,7 @@
         q = pl.ds(r * 128, 128)
         xt_ref[:, q] = x_ref[q, :].T
 
-    _skewed(ff // FW, first, act, second, [functools.partial(transpose, r) for r in range(tm // 128)])
+    _skewed(ff // FW, first, act, second, [functools.partial(transpose, r) for r in range(tm // 128)], True)
     _flush(acc_ref, dw1_ref, sem)
 
 
@@ -266,9 +268,9 @@
         xf, gf = x.reshape(-1, d), g.reshape(-1, d)
         gather = functools.partial(lax.all_gather, axis_name=AX, axis=0, tiled=True)
         scatter = functools.partial(lax.psum_scatter, axis_name=AX, scatter_dimension=0, tiled=True)
-        v1a = _gather(w1, HEAD)
-        v1a, w1b, w2 = lax.optimization_barrier((v1a, w1[0, :, HEAD:], w2))
-        v1b, v2 = gather(w1b), gather(w2[0])
+        v1a, w1b = _gather(w1, HEAD)
+        w1b, w2 = lax.optimization_barrier((w1b, w2))
+        v1b, v2 = gather(w1b[0]), gather(w2[0])
         rows = v2.shape[0]
         a0, h0, p2 = _fwd(xf, gf, v1a, 0, 0, rows, 2 * TM)
         a1, h1, p2 = _fwd(xf, gf, v1b, 0, HEAD, rows, TM, p2)

time: 493 us -> 486 us (0.986)
  Pallas kernels: 476 us -> 471 us
    pallas_call x1, Pallas kernels: 187 us -> 182 us  [_bwd(): pl.pallas_call(_bwd_kernel, grid=(t // TM,), in_specs=[token(d), token(d)...]
  transfers between devices with their start and end apart: 4 -> 4, of which waited for: 0 -> 0; matrix products, arithmetic and copies ran while one was open for 0% -> 0% of each run, Pallas kernels for 93% -> 94%
where the time goes in v4:
time: 486 us
  Pallas kernels  471 us (97%)
  between operations  13.8 us (3%)
    pallas_call x2, Pallas kernels, _fwd(): pl.pallas_call(functools.partial(_fwd_kernel, row0, col0), grid=(t // tm,...  184 us
    pallas_call x1, Pallas kernels, _bwd(): pl.pallas_call(_bwd_kernel, grid=(t // TM,), in_specs=[token(d), token(d)...  182 us
    pallas_call x1, Pallas kernels, _out(): pl.pallas_call(_out_kernel, grid=(t // TM,), in_specs=[token(d), token(h0...  87.9 us
    pallas_call x1, Pallas kernels, _gather(): pl.pallas_call(_gather_kernel, in_specs=[vmem], out_specs=[vmem, vmem], o...  16.5 us
  transfers between devices with their start and end apart: 4, of which 0 were waited for; matrix products, arithmetic and copies ran while one was open for 0% of the time, Pallas kernels for 94%

profile of v4, /device:TPU:0, one launch (start us, length us, event | category | flops | bytes accessed | tf_op | source)
XLA Modules:
  0.0 485.6 jit_solution(4920038622326234556)
XLA Ops:
  7.2 0.0 all-gather.5.cloned.1.call-start
  7.2 16.5 %gather.1 = (bf16[16,48,768]{2,1,0:T(8,128)(2,1)}, bf16[1,48,2304]{2,1,0:T(8,128)(2,1)}) custom-call(bf16[1,48,3072]{2,1,0:T(8,128)(2,1)} %w_ref.1), custom_call_target="tpu_custom_call" | custom-call | tf_op jit(solution)/shard_map/gather/pallas_call | solution.py:85
  23.7 0.0 all-gather.5.cloned.1.call-update
  23.8 0.0 all-gather.7.cloned.1.call-start
  23.8 0.7 all-gather.7.cloned.1.call-update
  24.5 0.0 reduce-scatter.5.cloned.1.call-start
  24.6 49.4 %fwd.2 = (bf16[16384,768]{1,0:T(8,128)(2,1)}, bf16[16384,768]{1,0:T(8,128)(2,1)}, f32[3072,768]{1,0:T(8,128)}) custom-call(bf16[16384,768]{1,0:T(8,128)(2,1)} %bitcast.11, bf16[16384,768]{1,0:T(8,128)(2,1)} %bitcast.8, bf16[768,768]{1,0:T(8,128)(2,1)} %bitcast.18), custom_call_target="tpu_custom_call" | custom-call | flops 38654705664 | bytes 100663296 | tf_op jit(solution)/shard_map/fwd/pallas_call | solution.py:162
  74.0 0.0 all-gather.5.cloned.1.call-done
  74.0 134.8 %fwd.3 = (bf16[16384,2304]{1,0:T(8,128)(2,1)}, bf16[16384,2304]{1,0:T(8,128)(2,1)}, f32[3072,768]{1,0:T(8,128)}) custom-call(bf16[16384,768]{1,0:T(8,128)(2,1)} %bitcast.12, bf16[16384,768]{1,0:T(8,128)(2,1)} %bitcast.9, bf16[768,2304]{1,0:T(8,128)(2,1)} %bitcast.17, f32[3072,768]{1,0:T(8,128)} %get-tuple-element.19.refs_3_), custom_call_target="tpu_custom_call", output_to_operand_aliasing={{2}: (3, {})} | custom-call | flops 115964116992 | bytes 201326592 | tf_op jit(solution)/shard_map/fwd/pallas_call | solution.py:162
  208.8 0.0 reduce-scatter.5.cloned.1.call-update
  208.9 0.2 reduce-scatter.3.cloned.1.call-start
  209.1 0.0 all-gather.7.cloned.1.call-done
  209.1 182.0 %bwd.1 = f32[768,3072]{1,0:T(8,128)} custom-call(bf16[16384,768]{1,0:T(8,128)(2,1)} %bitcast.13, bf16[16384,768]{1,0:T(8,128)(2,1)} %bitcast.10, bf16[16384,768]{1,0:T(8,128)(2,1)} %get-tuple-element.21.a0_ref, bf16[16384,2304]{1,0:T(8,128)(2,1)} %get-tuple-element.22.a1_ref, bf16[3072,768]{1,0:T(8,128)(2,1)} %bitcast.15), custom_call_target="tpu_custom_call" | custom-call | flops 154618822656 | bytes 150994944 | tf_op jit(solution)/shard_map/bwd/pallas_call | solution.py:224
  391.1 0.0 reduce-scatter.3.cloned.1.call-update
  391.1 87.9 %out.1 = bf16[16384,768]{1,0:T(8,128)(2,1)} custom-call(bf16[16384,768]{1,0:T(8,128)(2,1)} %bitcast.14, bf16[16384,768]{1,0:T(8,128)(2,1)} %get-tuple-element.24.h0_ref, bf16[16384,2304]{1,0:T(8,128)(2,1)} %get-tuple-element.25.h1_ref, bf16[3072,768]{1,0:T(8,128)(2,1)} %bitcast.16), custom_call_target="tpu_custom_call" | custom-call | flops 77309411328 | bytes 150994944 | tf_op jit(solution)/shard_map/out/pallas_call | solution.py:250
  479.1 0.0 reduce-scatter.5.cloned.1.call-done
  479.1 0.0 reduce-scatter.3.cloned.1.call-done
Async XLA Ops:
  7.2 66.8 %all-gather.5.cloned.1.call-start = ((), (), s32[]{:S(2)}) async-start(), calls=%async_computation.4 | async-start | bytes 3760128 | tf_op jit(solution)/shard_map/all_gather | solution.py:273
  23.8 185.4 %all-gather.7.cloned.1.call-start = ((), (), s32[]{:S(2)}) async-start(), calls=%async_computation.5 | async-start | bytes 5013504 | tf_op jit(solution)/shard_map/all_gather | solution.py:273
  24.5 454.6 %reduce-scatter.5.cloned.1.call-start = ((), (), s32[]{:S(2)}) async-start(), calls=%async_computation.3 | async-start | bytes 10027008 | tf_op jit(solution)/shard_map/reduce_scatter | solution.py:277
  208.9 270.2 %reduce-scatter.3.cloned.1.call-start = ((), (), s32[]{:S(2)}) async-start(), calls=%async_computation.2 | async-start | bytes 10027008 | tf_op jit(solution)/shard_map/reduce_scatter | solution.py:279
Sparse Core Ops, SparseCore 0:
  23.9 33.0 all-gather.4
  59.2 36.6 all-gather.6
  209.0 79.6 reduce-scatter.4
  391.2 79.7 reduce-scatter.2
